TPU v7x, 32 devices: a whole 2x2x4 slice. The times are simulated.
32 devices in a mesh: tm: 4 (over y, x), sky: 8 (over z, core).
Axes of the slice: x: 2, y: 2, z: 4, core: 2. Of those that a mesh axis runs over, the one named last changes fastest.
Arguments:
- residual: float32 [16384, 128], P(('tm', 'sky')), may hold values from -110 to 110
- obs_weight: float32 [16384, 128], P(('tm', 'sky')), may hold values from 0.5 to 2
- source_partials: float32 [5, 16384, 128], P(None, ('tm', 'sky')), may hold values from -1 to 1
- attitude_partials: float32 [16, 16384, 128], P(None, ('tm', 'sky')), may hold values from -1.5 to 1.5
- source_index: int32 [16384, 128], P(('tm', 'sky')), may hold values from 0 to 127
- tile_pixel: int32 [16384], P(('tm', 'sky')), may hold values from 0 to 1023, as said below
- tile_knot: int32 [16384], P(('tm', 'sky')), may hold values from 0 to 2047, as said below
- pixel_slot: int32 [1024], replicated, may hold values from 0 to 1023, as said below
Outputs:
- final_residual: float32 [16384, 128], P(('tm', 'sky'))
- source_update: float32 [5, 131072], P(None, 'sky')
- attitude_update: float32 [4, 2048], P(None, 'tm')
Inputs may be any that keep to these rules, and one draw needn't show every extreme that they name: Tiles come in aligned blocks of 512; with owner = pixel_slot[tile_pixel[t]] // 128, no block holds more than 192 tiles of one owner, and every block holds exactly 192 tiles of some owner. `pixel_slot`: every slot number appears once. `tile_knot`: the tiles of aligned block q of 512 tiles have first knots in [q * 64, (q + 1) * 64).
All inputs are finite; a program needn't handle non-finite values.
Results may differ from a plain program's by a relative error of at most 0.0003.
Values sent between devices are 32-bit elements; how exact they have to be, the bound alone decides.
No kernel may reach another device: no remote copies, remote signals or barrier semaphores. Data moves between devices by JAX's collectives and lax.ppermute only.
A program may use at most 128 MiB of HBM per device.

v0:
```python
import math
import jax
import jax.numpy as jnp
from jax import lax
from jax.sharding import PartitionSpec as P

PIX_DEV = 128
SRC_PIX = 128
KNOTS_DEV = 512
SOURCE_PAIRS = tuple(((first, second) for first in range(5) for second in range(first, 5)))
KNOT_PAIRS = tuple(((first, second) for first in range(4) for second in range(first, 4)))


def passed_along(value, axis, steps):
    count = lax.axis_size(axis)
    first, last = (max(0, -steps), min(count, count - steps))
    return lax.ppermute(value, axis, [(source, source + steps) for source in range(first, last)])


def damped_solve(normal, target, order, pairs):
    entries = {}
    for number, couple in enumerate(pairs):
        entries[couple] = normal[number]
    factor = {}
    for column in range(order):
        pivot_value = entries[column, column] + 1.0
        for earlier in range(column):
            pivot_value = pivot_value - factor[column, earlier] * factor[column, earlier]
        pivot_value = jnp.sqrt(pivot_value)
        factor[column, column] = pivot_value
        for below in range(column + 1, order):
            current = entries[column, below]
            for earlier in range(column):
                current = current - factor[below, earlier] * factor[column, earlier]
            factor[below, column] = current / pivot_value
    forward = []
    for column in range(order):
        current = target[column]
        for earlier in range(column):
            current = current - factor[column, earlier] * forward[earlier]
        forward.append(current / factor[column, column])
    answer = [None] * order
    for column in reversed(range(order)):
        current = forward[column]
        for later in range(column + 1, order):
            current = current - factor[later, column] * answer[later]
        answer[column] = current / factor[column, column]
    return jnp.stack(answer)


def knot_terms(weights, partials, baseline):
    result = []
    for segment in range(4):
        portion = partials[4 * segment : 4 * segment + 4]
        sums_rows = [
            jnp.sum(weights * portion[first] * portion[second], axis=-1)
            for first, second in KNOT_PAIRS
        ]
        sums_rows = sums_rows + [
            jnp.sum(weights * portion[first] * baseline, axis=-1) for first in range(4)
        ]
        result.append(jnp.stack(sums_rows))
    return result


def correct(baseline, partials, picked):
    accumulated = partials[0] * picked[0]
    for component in range(1, partials.shape[0]):
        accumulated = accumulated + partials[component] * picked[component]
    return baseline - accumulated


def pixel_sums(products, indices, owners, capacity):

    def add_sender(sender, running):
        offset = sender * capacity
        portion = lax.dynamic_slice_in_dim(products, offset, capacity, 1)
        chosen = lax.dynamic_slice_in_dim(indices, offset, capacity, 0)
        within = ((chosen % SRC_PIX)[:, :, None] == jnp.arange(SRC_PIX, dtype=jnp.int32)).astype(
            jnp.float32
        )
        pixel_hits = (
            (chosen[:, 0] // SRC_PIX)[:, None] == jnp.arange(PIX_DEV, dtype=jnp.int32)
        ).astype(jnp.float32)
        spread = jnp.einsum("ctk,tks->cts", portion, within, precision=lax.Precision.HIGHEST)
        return running + jnp.einsum(
            "cts,tp->cps", spread, pixel_hits, precision=lax.Precision.HIGHEST
        )

    running = lax.fori_loop(0, owners, add_sender, jnp.zeros((20, PIX_DEV, SRC_PIX), jnp.float32))
    return running.reshape(20, PIX_DEV * SRC_PIX)


def pick_sources(update, indices, rows):
    pixels = update.shape[1] // SRC_PIX
    table = update.reshape(update.shape[0], pixels, SRC_PIX)
    blocks = indices.shape[0] // rows

    def fill(number, output):
        offset = number * rows
        chosen = lax.dynamic_slice_in_dim(indices, offset, rows, 0)
        pixel_hits = (
            (chosen[:, 0] // SRC_PIX)[:, None] == jnp.arange(pixels, dtype=jnp.int32)
        ).astype(jnp.float32)
        within = ((chosen % SRC_PIX)[:, :, None] == jnp.arange(SRC_PIX, dtype=jnp.int32)).astype(
            jnp.float32
        )
        row_values = jnp.einsum("tp,cps->cts", pixel_hits, table, precision=lax.Precision.HIGHEST)
        picked = jnp.einsum("cts,tks->ctk", row_values, within, precision=lax.Precision.HIGHEST)
        return lax.dynamic_update_slice_in_dim(output, picked, offset, 1)

    empty = jnp.zeros((update.shape[0], indices.shape[0], indices.shape[1]), jnp.float32)
    return lax.fori_loop(0, blocks, fill, empty)


def body(
    residual,
    obs_weight,
    source_partials,
    attitude_partials,
    source_index,
    tile_pixel,
    tile_knot,
    pixel_slot,
):
    owners = lax.axis_size("sky")
    tiles = residual.shape[0]
    capacity = 3 * tiles // owners
    pixels = pixel_slot.shape[0]
    pixel_match = (tile_pixel[:, None] == jnp.arange(pixels, dtype=jnp.int32)[None, :]).astype(
        jnp.float32
    )
    seats_float = jnp.dot(
        pixel_match, pixel_slot.astype(jnp.float32), precision=lax.Precision.HIGHEST
    )
    seats = seats_float.astype(jnp.int32)
    owner_ids = seats // PIX_DEV
    local_pixel = seats % PIX_DEV
    member = (owner_ids[:, None] == jnp.arange(owners, dtype=jnp.int32)[None, :]).astype(
        jnp.float32
    )
    tile_numbers = jnp.arange(tiles, dtype=jnp.int32)
    lower = (tile_numbers[:, None] > tile_numbers[None, :]).astype(jnp.float32)
    before = jnp.dot(lower, member, precision=lax.Precision.HIGHEST)
    position = jnp.sum(before * member, axis=1).astype(jnp.int32)
    slot_index = owner_ids * capacity + position
    place = (jnp.arange(owners * capacity, dtype=jnp.int32)[:, None] == slot_index[None, :]).astype(
        jnp.float32
    )
    local_source = (local_pixel[:, None] * SRC_PIX + source_index).astype(jnp.float32)
    sent_index = jnp.dot(place, local_source, precision=lax.Precision.HIGHEST).astype(jnp.int32)[
        None
    ]
    root_weight = jnp.sqrt(obs_weight)
    fields = jnp.concatenate(
        [(root_weight * residual)[None], root_weight[None] * source_partials], axis=0
    )
    packed = jnp.einsum("st,ctk->csk", place, fields, precision=lax.Precision.HIGHEST)
    arrived, arrived_index = (
        lax.all_to_all(packed, "sky", split_axis=1, concat_axis=1, tiled=True),
        lax.all_to_all(sent_index, "sky", split_axis=1, concat_axis=1, tiled=True),
    )
    scaled = arrived[1:]
    products = [scaled[first] * scaled[second] for first, second in SOURCE_PAIRS]
    products = jnp.stack(products + [scaled[first] * arrived[0] for first in range(5)])
    normals = pixel_sums(products, arrived_index[0], owners, capacity)
    summed = lax.psum(normals, "tm")
    source_update = damped_solve(summed[:15], summed[15:], 5, SOURCE_PAIRS)
    everything = lax.all_gather(source_update, "sky", axis=1, tiled=True)
    global_source = seats[:, None] * SRC_PIX + source_index
    picked = pick_sources(everything, global_source, math.gcd(tiles, 64))
    settled = correct(residual, source_partials, picked)
    knot_start = tile_knot - lax.axis_index("tm") * KNOTS_DEV
    knot_hits = (knot_start[:, None] == jnp.arange(KNOTS_DEV, dtype=jnp.int32)[None, :]).astype(
        jnp.float32
    )
    accumulated = jnp.zeros((14, KNOTS_DEV + 3), jnp.float32)
    for segment, tile_sums in enumerate(knot_terms(obs_weight, attitude_partials, settled)):
        placed = jnp.dot(tile_sums, knot_hits, precision=lax.Precision.HIGHEST)
        accumulated = accumulated + jnp.pad(placed, ((0, 0), (segment, 3 - segment)))
    arriving = passed_along(accumulated[:, KNOTS_DEV:], "tm", 1)
    own_rows = accumulated[:, :KNOTS_DEV] + jnp.pad(arriving, ((0, 0), (0, KNOTS_DEV - 3)))
    whole = lax.psum(own_rows, "sky")
    attitude_update = damped_solve(whole[:10], whole[10:], 4, KNOT_PAIRS)
    following = passed_along(attitude_update[:, :3], "tm", -1)
    extended = jnp.concatenate([attitude_update, following], axis=1)
    accumulated_fix = None
    for segment in range(4):
        window = extended[:, segment : segment + KNOTS_DEV]
        values = jnp.dot(window, knot_hits.T, precision=lax.Precision.HIGHEST)
        for component in range(4):
            addend = attitude_partials[4 * segment + component] * values[component][:, None]
            accumulated_fix = addend if accumulated_fix is None else accumulated_fix + addend
    final_residual = settled - accumulated_fix
    return (final_residual, source_update, attitude_update)


def solution(mesh):
    in_specs = (
        P(("tm", "sky"), None),
        P(("tm", "sky"), None),
        P(None, ("tm", "sky"), None),
        P(None, ("tm", "sky"), None),
        P(("tm", "sky"), None),
        P(("tm", "sky")),
        P(("tm", "sky")),
        P(),
    )
    out_specs = (P(("tm", "sky"), None), P(None, "sky"), P(None, "tm"))
    return jax.shard_map(body, mesh=mesh, in_specs=in_specs, out_specs=out_specs, check_vma=False)
```

profile of v0, /device:TPU:0, one launch (start us, length us, event | category | flops | bytes accessed | tf_op | source)
XLA Modules:
  0.0 626.5 jit_solution(8565217620249601764)
XLA Ops:
  12.9 6.0 convolution_bitcast_fusion.1
  18.8 6.2 copy.44
  25.0 6.5 %all-to-all-start.1 = ((f32[6,1536,128]{2,0,1:T(8,128)}), f32[6,1536,128]{2,0,1:T(8,128)}, u32[]{:S(2)}, u32[]{:S(2)}) async-start(f32[6,1536,128]{2,0,1:T(8,128)} %copy.44), calls=%async_computation.1 | async-start | bytes 12582912 | tf_op jit(solution)/shard_map/all_to_all | solution.py:160
  34.0 136.5 %all-to-all-done.1 = f32[6,1536,128]{2,0,1:T(8,128)} async-done(((f32[6,1536,128]{2,0,1:T(8,128)}), f32[6,1536,128]{2,0,1:T(8,128)}, u32[]{:S(2)}, u32[]{:S(2)}) %all-to-all-start.1) | async-done | bytes 4718624 | tf_op jit(solution)/shard_map/all_to_all | solution.py:160
  170.5 4.2 all-to-all-start
  175.0 22.1 %slice_multiply_fusion = (f32[1,1536,128]{2,0,1:T(1,128)S(1)}, f32[1,1536,128]{2,0,1:T(1,128)S(1)}, f32[1,1536,128]{2,0,1:T(1,128)}, f32[1,1536,128]{2,0,1:T(1,1...) fusion(f32[6,1536,128]{2,0,1:T(8,128)} %all-to-all-done.1), kind=kLoop, calls=%fused_computation.340 | loop fusion | flops 2359296 | bytes 14155776 | tf_op jit(solution)/shard_map/mul | solution.py:165
  197.1 20.9 %slice_multiply_fusion.1 = (f32[1,1536,128]{2,0,1:T(1,128)}, f32[1,1536,128]{2,0,1:T(1,128)}, f32[1,1536,128]{2,0,1:T(1,128)}, f32[1,1536,128]{2,0,1:T(1,128)}, ...) fusion(f32[6,1536,128]{2,0,1:T(8,128)} %all-to-all-done.1), kind=kLoop, calls=%fused_computation.341 | loop fusion | flops 1572864 | bytes 11010048 | tf_op jit(solution)/shard_map/mul | solution.py:165
  218.0 49.6 %stack.218 = f32[20,1536,128]{2,0,1:T(8,128)} concatenate(f32[1,1536,128]{2,0,1:T(1,128)} %get-tuple-element.400, f32[1,1536,128]{2,0,1:T(1,128)} %get-tuple-element.408, f32[1,1536,128]{2,0,1:T(1,128)} %get-tuple-element.407, f32[1,1536,128]{2,0,1:T(1,128)} %get-tuple-element.406, f32[1,1536,128]{2,0,1:T(1,128)} %get-tuple-element.405, f32[1,1536,128]{2,0,1:T(1,128)S(1)} %get-tuple-element.390, ...), dimensions={0} | concatenate | bytes 31457280 | tf_op jit(solution)/shard_map/stack | solution.py:165
  267.7 114.9 %while.32 = (s32[]{:T(128)}, f32[20,128,128]{2,1,0:T(8,128)S(1)}, s32[1536,128]{1,0:T(8,128)}, f32[20,1536,128]{2,0,1:T(8,128)}, s32[]{:T(128)}, /*index=5*/s32[]{:T(128)}, s32[]{:T(128)}, s32[]{:T(128)}) while((s32[]{:T(128)}, f32[20,128,128]{2,1,0:T(8,128)S(1)}, s32[1536,128]{1,0:T(8,128)}, f32[20,1536,128]{2,0,1:T(8,128)}, ...), condition=%wide.region_2.3_spmd.clone, body=%wide.region_1.2_spmd.clone.sunk | while | flops 1514048256 | bytes 9800085 | solution.py:90
  268.8 9.9 %fusion.206 = f32[20,192,128]{2,0,1:T(8,128)} fusion(f32[20,1536,128]{2,0,1:T(8,128)} %get-tuple-element.501, s32[]{:T(128)S(6)} %select_n.124, s32[192,128]{1,0:T(8,128)S(1)} %copy.140), kind=kOutput, calls=%fused_computation.26.clone.1 | convolution fusion | flops 758120448 | bytes 4423684 | tf_op jit(solution)/shard_map/while/body/eval_jaxpr/ctk,tks->cts/dot_general | solution.py:85
  283.2 9.9 %fusion.206 = f32[20,192,128]{2,0,1:T(8,128)} fusion(f32[20,1536,128]{2,0,1:T(8,128)} %get-tuple-element.501, s32[]{:T(128)S(6)} %select_n.124, s32[192,128]{1,0:T(8,128)S(1)} %copy.140), kind=kOutput, calls=%fused_computation.26.clone.1 | convolution fusion | flops 758120448 | bytes 4423684 | tf_op jit(solution)/shard_map/while/body/eval_jaxpr/ctk,tks->cts/dot_general | solution.py:85
  297.6 9.9 %fusion.206 = f32[20,192,128]{2,0,1:T(8,128)} fusion(f32[20,1536,128]{2,0,1:T(8,128)} %get-tuple-element.501, s32[]{:T(128)S(6)} %select_n.124, s32[192,128]{1,0:T(8,128)S(1)} %copy.140), kind=kOutput, calls=%fused_computation.26.clone.1 | convolution fusion | flops 758120448 | bytes 4423684 | tf_op jit(solution)/shard_map/while/body/eval_jaxpr/ctk,tks->cts/dot_general | solution.py:85
  311.9 9.9 %fusion.206 = f32[20,192,128]{2,0,1:T(8,128)} fusion(f32[20,1536,128]{2,0,1:T(8,128)} %get-tuple-element.501, s32[]{:T(128)S(6)} %select_n.124, s32[192,128]{1,0:T(8,128)S(1)} %copy.140), kind=kOutput, calls=%fused_computation.26.clone.1 | convolution fusion | flops 758120448 | bytes 4423684 | tf_op jit(solution)/shard_map/while/body/eval_jaxpr/ctk,tks->cts/dot_general | solution.py:85
  326.3 9.9 %fusion.206 = f32[20,192,128]{2,0,1:T(8,128)} fusion(f32[20,1536,128]{2,0,1:T(8,128)} %get-tuple-element.501, s32[]{:T(128)S(6)} %select_n.124, s32[192,128]{1,0:T(8,128)S(1)} %copy.140), kind=kOutput, calls=%fused_computation.26.clone.1 | convolution fusion | flops 758120448 | bytes 4423684 | tf_op jit(solution)/shard_map/while/body/eval_jaxpr/ctk,tks->cts/dot_general | solution.py:85
  340.6 9.9 %fusion.206 = f32[20,192,128]{2,0,1:T(8,128)} fusion(f32[20,1536,128]{2,0,1:T(8,128)} %get-tuple-element.501, s32[]{:T(128)S(6)} %select_n.124, s32[192,128]{1,0:T(8,128)S(1)} %copy.140), kind=kOutput, calls=%fused_computation.26.clone.1 | convolution fusion | flops 758120448 | bytes 4423684 | tf_op jit(solution)/shard_map/while/body/eval_jaxpr/ctk,tks->cts/dot_general | solution.py:85
  355.0 9.9 %fusion.206 = f32[20,192,128]{2,0,1:T(8,128)} fusion(f32[20,1536,128]{2,0,1:T(8,128)} %get-tuple-element.501, s32[]{:T(128)S(6)} %select_n.124, s32[192,128]{1,0:T(8,128)S(1)} %copy.140), kind=kOutput, calls=%fused_computation.26.clone.1 | convolution fusion | flops 758120448 | bytes 4423684 | tf_op jit(solution)/shard_map/while/body/eval_jaxpr/ctk,tks->cts/dot_general | solution.py:85
  369.4 9.9 %fusion.206 = f32[20,192,128]{2,0,1:T(8,128)} fusion(f32[20,1536,128]{2,0,1:T(8,128)} %get-tuple-element.501, s32[]{:T(128)S(6)} %select_n.124, s32[192,128]{1,0:T(8,128)S(1)} %copy.140), kind=kOutput, calls=%fused_computation.26.clone.1 | convolution fusion | flops 758120448 | bytes 4423684 | tf_op jit(solution)/shard_map/while/body/eval_jaxpr/ctk,tks->cts/dot_general | solution.py:85
  385.1 61.7 %all-reduce.7.cloned.1.call-done = f32[20,16384]{1,0:T(8,128)} async-done(((f32[20,16384]{1,0:T(8,128)}), f32[20,16384]{1,0:T(8,128)}) %all-reduce.7.cloned.1.call-update) | async-done | bytes 1310736 | tf_op jit(solution)/shard_map/psum | solution.py:167
  446.8 5.2 fusion.141
  468.1 40.0 %all-gather.2.cloned.1.call-done = f32[5,131072]{1,0:T(8,128)} async-done(((f32[5,16384]{1,0:T(8,128)}), f32[5,131072]{1,0:T(8,128)}) %all-gather.2.cloned.1.call-update) | async-done | bytes 2621456 | tf_op jit(solution)/shard_map/all_gather | solution.py:169
  511.9 55.2 %while.31 = (s32[]{:T(128)}, f32[5,512,128]{2,1,0:T(8,128)}, s32[512,128]{0,1:T(8,128)S(1)}, f32[5,1024,128]{2,1,0:T(8,128)S(1)}, s32[]{:T(128)}, /*index=5*/s32[]{:T(128)}, s32[]{:T(128)}, s32[]{:T(128)}) while((s32[]{:T(128)}, f32[5,512,128]{2,1,0:T(8,128)}, s32[512,128]{0,1:T(8,128)S(1)}, f32[5,1024,128]{2,1,0:T(8,128)S(1)}, s32[]{:T(128)}, ...), condition=%wide.region_5.6_spmd, body=%wide.region_4.5_spmd.sunk | while | flops 567436224 | bytes 3605391 | solution.py:113
  513.4 4.8 fusion.202
  520.2 4.8 fusion.202
  527.1 4.8 fusion.202
  534.1 4.8 fusion.202
  541.0 4.8 fusion.202
  547.8 4.8 fusion.202
  554.8 4.8 fusion.202
  561.7 4.8 fusion.202
  580.5 25.9 %psum.15 = f32[14,512]{1,0:T(8,128)S(1)} all-reduce(f32[14,512]{1,0:T(8,128)S(1)} %slice_add_fusion.5), channel_id=1, replica_groups=mesh['tm'=4,'sky'=8] {'sky'}, use_global_device_ids=true, to_apply=%region_62.63 | all-reduce | flops 7168 | bytes 57344 | tf_op jit(solution)/shard_map/psum | solution.py:183
  608.6 4.4 collective-permute-done.1
  615.0 4.6 fusion.61
  (169 shorter events, 100.1 us)
Async XLA Ops:
  7.2 5.1 copy-start.1
  25.0 6.5 %copy-start.8 = (s32[512,128]{1,0:T(8,128)S(1)}, s32[512,128]{1,0:T(8,128)}, u32[]{:S(2)}) copy-start(s32[512,128]{1,0:T(8,128)} %param.16) | copy-start | bytes 786436
  25.0 145.5 %all-to-all-start.1 = ((f32[6,1536,128]{2,0,1:T(8,128)}), f32[6,1536,128]{2,0,1:T(8,128)}, u32[]{:S(2)}, u32[]{:S(2)}) async-start(f32[6,1536,128]{2,0,1:T(8,128)} %copy.44), calls=%async_computation.1 | async-start | bytes 12582912 | tf_op jit(solution)/shard_map/all_to_all | solution.py:160
  170.5 97.1 %all-to-all-start = ((s32[1,1536,128]{2,0,1:T(1,128)}), s32[1,1536,128]{2,0,1:T(1,128)}, u32[]{:S(2)}, u32[]{:S(2)}) async-start(s32[1,1536,128]{2,0,1:T(1,128)} %bitcast.7), calls=%async_computation | async-start | bytes 1572864 | tf_op jit(solution)/shard_map/all_to_all | solution.py:161
  174.7 272.1 %all-reduce.7.cloned.1.call-start = ((), (), s32[]{:S(2)}) async-start(), calls=%async_computation.2 | async-start | bytes 3145728 | tf_op jit(solution)/shard_map/psum | solution.py:167
  384.8 123.3 %all-gather.2.cloned.1.call-start = ((), (), s32[]{:S(2)}) async-start(), calls=%async_computation.3 | async-start | bytes 4718592 | tf_op jit(solution)/shard_map/all_gather | solution.py:169
  456.0 5.2 copy-start.10
  456.0 5.3 copy-start.2
  567.1 3.7 copy-start
  567.1 3.7 copy-start.3
  567.1 3.8 copy-start.4
  567.1 3.9 copy-start.5
  567.1 3.9 copy-start.6
  567.1 4.0 copy-start.7
  575.8 4.7 collective-permute-start
  606.6 13.0 %copy-start.9 = (f32[4,512]{1,0:T(4,128)}, f32[4,512]{1,0:T(4,128)S(1)}, u32[]{:S(2)}) copy-start(f32[4,512]{1,0:T(4,128)S(1)} %pad_maximum_fusion.1) | copy-start | bytes 24580
  607.3 5.7 collective-permute-start.1
Sparse Core Ops, SparseCore 0:
  384.9 61.8 all-reduce.6
  461.2 46.8 all-gather.1
where the time goes:
time: 634 us; the launch traced here: 626 us
  waiting for transfers between devices  244 us (38%)
  matrix products  168 us (26%)
  local copies, waits for them, and re-layouts  81.4 us (13%)
  other arithmetic  76.7 us (12%)
  blocking collectives  25.9 us (4%)
  starting transfers between devices  15.8 us (2%)
  between operations  14.4 us (2%)
    all_to_all x1, waiting for transfers between devices, body(): lax.all_to_all(packed, 'sky', split_axis=1, concat_axis=1, tiled=True)  137 us
    dot_general x8, matrix products, add_sender(): jnp.einsum('ctk,tks->cts', portion, within, precision=lax.Precision.HIGHEST)  79.5 us
    psum x1, waiting for transfers between devices, body(): summed = lax.psum(normals, 'tm')  61.7 us
    another operation x1, local copies, waits for them, and re-layouts, body(): jnp.stack(products + [scaled[first] * arrived[0] for first in range(5)])  49.6 us
    mul x2, other arithmetic, body(): scaled[first] * arrived[0]  43.1 us
    all_gather x1, waiting for transfers between devices, body(): everything = lax.all_gather(source_update, 'sky', axis=1, tiled=True)  40 us
    dot_general x8, matrix products, fill(): jnp.einsum('cts,tks->ctk', row_values, within, precision=lax.Precision.HI...  38 us
    psum x1, blocking collectives, body(): whole = lax.psum(own_rows, 'sky')  25.9 us
  transfers between devices with their start and end apart: 6, of which 5 were waited for; matrix products, arithmetic and copies ran while one was open for 16% of the time, Pallas kernels for 0%

commit v1 on v0

--- a/solution.py
+++ b/solution.py
@@ -157,7 +157,10 @@
     )
     packed = jnp.einsum("st,ctk->csk", place, fields, precision=lax.Precision.HIGHEST)
     arrived, arrived_index = (
-        lax.all_to_all(packed, "sky", split_axis=1, concat_axis=1, tiled=True),
+        jnp.concatenate(
+            lax.all_to_all(jnp.stack(jnp.split(packed, lax.axis_size("sky"), axis=1)), "sky", 0, 0),
+            axis=1,
+        ),
         lax.all_to_all(sent_index, "sky", split_axis=1, concat_axis=1, tiled=True),
     )
     scaled = arrived[1:]

time: 634 us -> 544 us (0.86); the launches traced: 626 us -> 543 us
  other arithmetic: 76.7 us -> 36 us
  waiting for transfers between devices: 244 us -> 211 us
  local copies, waits for them, and re-layouts: 81.4 us -> 69.9 us
    another operation x1, local copies, waits for them, and re-layouts: 49.6 us -> 0.94 us  [body(): jnp.stack(products + [scaled[first] * arrived[0] for first in range(5)])]
    mul x2, other arithmetic: 43.1 us -> 2.1 us  [body(): scaled[first] * arrived[0]]
    all_to_all x1, waiting for transfers between devices: 137 us -> 103 us  [body(): lax.all_to_all(jnp.stack(jnp.split(packed, lax.axis_size('sky'), axis=1))...]
    unnamed x29 -> x43, local copies, waits for them, and re-layouts: 8.03 us -> 34.4 us
    dynamic_slice x0 -> x8, local copies, waits for them, and re-layouts: none -> 13.8 us  [add_sender(): portion = lax.dynamic_slice_in_dim(products, offset, capacity, 1)]
    another operation x0 -> x2, local copies, waits for them, and re-layouts: none -> 7.39 us  [body(): jnp.stack(jnp.split(packed, lax.axis_size('sky'), axis=1))]
    dynamic_slice x16, local copies, waits for them, and re-layouts: 8 us -> 0.86 us  [add_sender(): chosen = lax.dynamic_slice_in_dim(indices, offset, capacity, 0)]
  transfers between devices with their start and end apart: 6 -> 6, of which waited for: 5 -> 5; matrix products, arithmetic and copies ran while one was open for 16% -> 6% of each run, Pallas kernels for 0% -> 0%
where the time goes in v1:
time: 544 us; the launch traced here: 543 us
  waiting for transfers between devices  211 us (39%)
  matrix products  171 us (31%)
  local copies, waits for them, and re-layouts  69.9 us (13%)
  other arithmetic  36 us (7%)
  blocking collectives  25.9 us (5%)
  starting transfers between devices  15 us (3%)
  between operations  14.4 us (3%)
    all_to_all x1, waiting for transfers between devices, body(): lax.all_to_all(jnp.stack(jnp.split(packed, lax.axis_size('sky'), axis=1))...  103 us
    dot_general x8, matrix products, add_sender(): jnp.einsum('ctk,tks->cts', portion, within, precision=lax.Precision.HIGHEST)  84.4 us
    psum x1, waiting for transfers between devices, body(): summed = lax.psum(normals, 'tm')  62 us
    all_gather x1, waiting for transfers between devices, body(): everything = lax.all_gather(source_update, 'sky', axis=1, tiled=True)  40 us
    dot_general x8, matrix products, fill(): jnp.einsum('cts,tks->ctk', row_values, within, precision=lax.Precision.HI...  38 us
    unnamed x43, local copies, waits for them, and re-layouts  34.4 us
    psum x1, blocking collectives, body(): whole = lax.psum(own_rows, 'sky')  25.9 us
    dot_general x8, matrix products, add_sender(): jnp.einsum('cts,tp->cps', spread, pixel_hits, precision=lax.Precision.HIG...  25.8 us
  transfers between devices with their start and end apart: 6, of which 5 were waited for; matrix products, arithmetic and copies ran while one was open for 6% of the time, Pallas kernels for 0%

profile of v1, /device:TPU:0, one launch (start us, length us, event | category | flops | bytes accessed | tf_op | source)
XLA Modules:
  0.0 543.1 jit_solution(17409122843602557673)
XLA Ops:
  14.1 4.1 convolution_bitcast_fusion.1
  26.7 6.2 %copy.62 = f32[8,6,192,128]{3,2,1,0:T(8,128)} copy(f32[8,6,192,128]{2,3,1,0:T(8,128)} %fusion.47) | data formatting | bytes 9437184 | tf_op jit(solution)/shard_map/stack | solution.py:161
  32.8 6.5 %all-to-all-start.1 = ((f32[8,6,192,128]{3,2,1,0:T(8,128)}), f32[8,6,192,128]{3,2,1,0:T(8,128)}, u32[]{:S(2)}, u32[]{:S(2)}) async-start(f32[8,6,192,128]{3,2,1,0:T(8,128)} %copy.62), calls=%async_computation.1 | async-start | bytes 9437184 | tf_op jit(solution)/shard_map/all_to_all | solution.py:161
  41.8 102.8 %all-to-all-done.1 = f32[8,6,192,128]{3,2,1,0:T(8,128)} async-done(((f32[8,6,192,128]{3,2,1,0:T(8,128)}), f32[8,6,192,128]{3,2,1,0:T(8,128)}, u32[]{:S(2)}, u32[]{:S(2)}) %all-to-all-start.1) | async-done | bytes 4718624 | tf_op jit(solution)/shard_map/all_to_all | solution.py:161
  172.2 126.6 %while.32 = (s32[]{:T(128)}, f32[20,128,128]{2,1,0:T(8,128)S(1)}, s32[1536,128]{1,0:T(8,128)S(1)}, f32[20,1536,128]{2,1,0:T(8,128)}, s32[]{:T(128)}, /*index=5*/s32[]{:T(128)}, s32[]{:T(128)}, s32[]{:T(128)}) while((s32[]{:T(128)}, f32[20,128,128]{2,1,0:T(8,128)S(1)}, s32[1536,128]{1,0:T(8,128)S(1)}, f32[20,1536,128]{2,1,0:T(8,128)}, ...), condition=%wide.region_2.3_spmd.clone, body=%wide.region_1.2_spmd.clone.sunk | while | flops 1514048256 | bytes 13339029 | solution.py:90
  174.2 10.5 %fusion.213 = f32[20,192,128]{2,0,1:T(8,128)} fusion(f32[20,192,128]{2,1,0:T(8,128)S(1)} %constant_dynamic-slice_fusion.5, s32[192,128]{1,0:T(8,128)S(1)} %copy.169), kind=kOutput, calls=%fused_computation.26.clone.1 | convolution fusion | flops 758120448 | bytes 4030464 | tf_op jit(solution)/shard_map/while/body/eval_jaxpr/ctk,tks->cts/dot_general | solution.py:85
  190.0 10.5 %fusion.213 = f32[20,192,128]{2,0,1:T(8,128)} fusion(f32[20,192,128]{2,1,0:T(8,128)S(1)} %constant_dynamic-slice_fusion.5, s32[192,128]{1,0:T(8,128)S(1)} %copy.169), kind=kOutput, calls=%fused_computation.26.clone.1 | convolution fusion | flops 758120448 | bytes 4030464 | tf_op jit(solution)/shard_map/while/body/eval_jaxpr/ctk,tks->cts/dot_general | solution.py:85
  205.9 10.5 %fusion.213 = f32[20,192,128]{2,0,1:T(8,128)} fusion(f32[20,192,128]{2,1,0:T(8,128)S(1)} %constant_dynamic-slice_fusion.5, s32[192,128]{1,0:T(8,128)S(1)} %copy.169), kind=kOutput, calls=%fused_computation.26.clone.1 | convolution fusion | flops 758120448 | bytes 4030464 | tf_op jit(solution)/shard_map/while/body/eval_jaxpr/ctk,tks->cts/dot_general | solution.py:85
  221.7 10.5 %fusion.213 = f32[20,192,128]{2,0,1:T(8,128)} fusion(f32[20,192,128]{2,1,0:T(8,128)S(1)} %constant_dynamic-slice_fusion.5, s32[192,128]{1,0:T(8,128)S(1)} %copy.169), kind=kOutput, calls=%fused_computation.26.clone.1 | convolution fusion | flops 758120448 | bytes 4030464 | tf_op jit(solution)/shard_map/while/body/eval_jaxpr/ctk,tks->cts/dot_general | solution.py:85
  237.5 10.5 %fusion.213 = f32[20,192,128]{2,0,1:T(8,128)} fusion(f32[20,192,128]{2,1,0:T(8,128)S(1)} %constant_dynamic-slice_fusion.5, s32[192,128]{1,0:T(8,128)S(1)} %copy.169), kind=kOutput, calls=%fused_computation.26.clone.1 | convolution fusion | flops 758120448 | bytes 4030464 | tf_op jit(solution)/shard_map/while/body/eval_jaxpr/ctk,tks->cts/dot_general | solution.py:85
  253.4 10.5 %fusion.213 = f32[20,192,128]{2,0,1:T(8,128)} fusion(f32[20,192,128]{2,1,0:T(8,128)S(1)} %constant_dynamic-slice_fusion.5, s32[192,128]{1,0:T(8,128)S(1)} %copy.169), kind=kOutput, calls=%fused_computation.26.clone.1 | convolution fusion | flops 758120448 | bytes 4030464 | tf_op jit(solution)/shard_map/while/body/eval_jaxpr/ctk,tks->cts/dot_general | solution.py:85
  269.2 10.5 %fusion.213 = f32[20,192,128]{2,0,1:T(8,128)} fusion(f32[20,192,128]{2,1,0:T(8,128)S(1)} %constant_dynamic-slice_fusion.5, s32[192,128]{1,0:T(8,128)S(1)} %copy.169), kind=kOutput, calls=%fused_computation.26.clone.1 | convolution fusion | flops 758120448 | bytes 4030464 | tf_op jit(solution)/shard_map/while/body/eval_jaxpr/ctk,tks->cts/dot_general | solution.py:85
  285.0 10.5 %fusion.213 = f32[20,192,128]{2,0,1:T(8,128)} fusion(f32[20,192,128]{2,1,0:T(8,128)S(1)} %constant_dynamic-slice_fusion.5, s32[192,128]{1,0:T(8,128)S(1)} %copy.169), kind=kOutput, calls=%fused_computation.26.clone.1 | convolution fusion | flops 758120448 | bytes 4030464 | tf_op jit(solution)/shard_map/while/body/eval_jaxpr/ctk,tks->cts/dot_general | solution.py:85
  301.1 62.0 %all-reduce.7.cloned.1.call-done = f32[20,16384]{1,0:T(8,128)} async-done(((f32[20,16384]{1,0:T(8,128)}), f32[20,16384]{1,0:T(8,128)}) %all-reduce.7.cloned.1.call-update) | async-done | bytes 1310736 | tf_op jit(solution)/shard_map/psum | solution.py:170
  363.1 5.2 fusion.148
  368.4 3.9 fusion.149
  372.3 3.9 subtract_divide_fusion
  380.9 3.7 fusion.106
  384.6 40.0 %all-gather.2.cloned.1.call-done = f32[5,131072]{1,0:T(8,128)} async-done(((f32[5,16384]{1,0:T(8,128)}), f32[5,131072]{1,0:T(8,128)}) %all-gather.2.cloned.1.call-update) | async-done | bytes 2621456 | tf_op jit(solution)/shard_map/all_gather | solution.py:172
  428.4 55.2 %while.31 = (s32[]{:T(128)}, f32[5,512,128]{2,1,0:T(8,128)}, s32[512,128]{0,1:T(8,128)S(1)}, f32[5,1024,128]{2,1,0:T(8,128)S(1)}, s32[]{:T(128)}, /*index=5*/s32[]{:T(128)}, s32[]{:T(128)}, s32[]{:T(128)}) while((s32[]{:T(128)}, f32[5,512,128]{2,1,0:T(8,128)}, s32[512,128]{0,1:T(8,128)S(1)}, f32[5,1024,128]{2,1,0:T(8,128)S(1)}, s32[]{:T(128)}, ...), condition=%wide.region_5.6_spmd, body=%wide.region_4.5_spmd.sunk | while | flops 567436224 | bytes 3605391 | solution.py:113
  429.9 4.8 fusion.209
  436.8 4.8 fusion.209
  443.7 4.8 fusion.209
  450.6 4.8 fusion.209
  457.5 4.8 fusion.209
  464.4 4.8 fusion.209
  471.3 4.8 fusion.209
  478.2 4.8 fusion.209
  483.6 3.6 multiply_reduce_fusion.12
  497.1 25.9 %psum.15 = f32[14,512]{1,0:T(8,128)S(1)} all-reduce(f32[14,512]{1,0:T(8,128)S(1)} %slice_add_fusion.5), channel_id=1, replica_groups=mesh['tm'=4,'sky'=8] {'sky'}, use_global_device_ids=true, to_apply=%region_62.63 | all-reduce | flops 7168 | bytes 57344 | tf_op jit(solution)/shard_map/psum | solution.py:186
  525.2 4.4 collective-permute-done.1
  531.6 4.6 fusion.68
  (193 shorter events, 128.8 us)
Async XLA Ops:
  32.8 6.5 %copy-start.2 = (s32[512,128]{1,0:T(8,128)S(1)}, s32[512,128]{1,0:T(8,128)}, u32[]{:S(2)}) copy-start(s32[512,128]{1,0:T(8,128)} %param.16) | copy-start | bytes 786436
  32.8 111.8 %all-to-all-start.1 = ((f32[8,6,192,128]{3,2,1,0:T(8,128)}), f32[8,6,192,128]{3,2,1,0:T(8,128)}, u32[]{:S(2)}, u32[]{:S(2)}) async-start(f32[8,6,192,128]{3,2,1,0:T(8,128)} %copy.62), calls=%async_computation.1 | async-start | bytes 9437184 | tf_op jit(solution)/shard_map/all_to_all | solution.py:161
  144.7 27.6 %all-to-all-start = ((s32[1,1536,128]{2,0,1:T(1,128)}), s32[1,1536,128]{2,0,1:T(1,128)S(1)}, u32[]{:S(2)}, u32[]{:S(2)}) async-start(s32[1,1536,128]{2,0,1:T(1,128)} %bitcast.7), calls=%async_computation | async-start | bytes 1572864 | tf_op jit(solution)/shard_map/all_to_all | solution.py:164
  148.2 214.9 %all-reduce.7.cloned.1.call-start = ((), (), s32[]{:S(2)}) async-start(), calls=%async_computation.2 | async-start | bytes 3145728 | tf_op jit(solution)/shard_map/psum | solution.py:170
  298.8 78.9 %copy-start.4 = (s32[512]{0:T(512)S(1)}, s32[512]{0:T(512)}, u32[]{:S(2)}) copy-start(s32[512]{0:T(512)} %param.18) | copy-start | bytes 6148
  299.0 78.8 %copy-start.1 = (f32[512,128]{1,0:T(8,128)S(1)}, f32[512,128]{1,0:T(8,128)}, u32[]{:S(2)}) copy-start(f32[512,128]{1,0:T(8,128)} %param.13) | copy-start | bytes 786436
  301.1 123.5 %all-gather.2.cloned.1.call-start = ((), (), s32[]{:S(2)}) async-start(), calls=%async_computation.3 | async-start | bytes 4718592 | tf_op jit(solution)/shard_map/all_gather | solution.py:172
  483.6 3.7 copy-start
  492.3 4.7 collective-permute-start
  523.2 13.0 %copy-start.3 = (f32[4,512]{1,0:T(4,128)}, f32[4,512]{1,0:T(4,128)S(1)}, u32[]{:S(2)}) copy-start(f32[4,512]{1,0:T(4,128)S(1)} %pad_maximum_fusion.1) | copy-start | bytes 24580
  523.9 5.7 %collective-permute-start.1 = (f32[4,3]{1,0:T(4,128)S(1)}, f32[4,3]{1,0:T(4,128)S(1)}, u32[]{:S(2)}, u32[]{:S(2)}) collective-permute-start(f32[4,3]{1,0:T(4,128)S(1)} %slice.620), channel_id=1, source_target_pairs={{8,0},{16,8},{24,16},{9,1},{17,9},{25,17},{10,2},{18,10},{26,18},{... | collective-permute-start | bytes 152 | tf_op jit(solution)/shard_map/ppermute | solution.py:17
Sparse Core Ops, SparseCore 0:
  301.2 61.8 all-reduce.6
  377.7 46.8 all-gather.1
